TPU v7x, 512 devices: a whole 4x4x16 slice. The times are simulated.
512 devices in a mesh: dp: 4 (over x), seq: 16 (over z), feat: 8 (over y, core).
Axes of the slice: x: 4, y: 4, z: 16, core: 2. Of those that a mesh axis runs over, the one named last changes fastest.
Arguments:
- tokens: bfloat16 [65536, 2048], P(('dp', 'seq')), parts along dimension 0, may hold values from -6 to 6
- w_query: bfloat16 [2048, 256], P(None, 'feat'), may hold values from -0.125 to 0.125
- w_key: bfloat16 [2048, 256], P(None, 'feat'), may hold values from -0.125 to 0.125
- value_weight: bfloat16 [2048, 2048], P(None, 'feat'), may hold values from -0.125 to 0.125
- w_out: bfloat16 [2048, 2048], P(None, 'feat'), may hold values from -0.125 to 0.125
Outputs:
- mixed: bfloat16 [65536, 2048], P(('dp', 'seq'), 'feat'), parts along dimension 0
There are 4 independent parts, one for each index of `dp`. A program takes and returns all parts, laid end to end along the dimension named above; an argument that names none is the same for every part. Nothing has to cross between parts.
All inputs are finite; a program needn't handle non-finite values.
Results may differ from a plain program's by a relative error of at most 0.009.
Values may be sent and summed in bfloat16 or wider, within the bound.
A program may use at most 64 MiB of HBM per device.

v0:
```python
import jax
import jax.numpy as jnp
from jax import lax
from jax.sharding import PartitionSpec as P

DK = 16
DV = 128


def key_features(key_rows):
    as_float = key_rows.astype(jnp.float32)
    row_count = key_rows.shape[0]
    head_total = key_rows.shape[1]
    linear = jnp.transpose(as_float, (1, 2, 0))
    square = jnp.einsum("nha,nhb->habn", as_float, as_float).reshape(head_total, -1, row_count)
    ones_row = jnp.ones((head_total, 1, row_count), jnp.float32)
    return jnp.concatenate([ones_row, linear, square], axis=1).astype(jnp.bfloat16)


def query_features(query_rows):
    as_float = query_rows.astype(jnp.float32)
    row_count = query_rows.shape[0]
    head_total = query_rows.shape[1]
    linear = jnp.transpose(as_float, (1, 2, 0)) * 0.25
    square = jnp.einsum("nha,nhb->habn", as_float, as_float).reshape(head_total, -1, row_count) * (
        1.0 / 32.0
    )
    ones_row = jnp.ones((head_total, 1, row_count), jnp.float32)
    return jnp.concatenate([ones_row, linear, square], axis=1)


def local(tokens, w_query, w_key, value_weight, w_out):
    row_count = tokens.shape[0]
    local_heads = value_weight.shape[1] // DV
    query_rows = (
        jnp.dot(tokens, w_query, preferred_element_type=jnp.float32)
        .astype(jnp.bfloat16)
        .reshape(row_count, local_heads, DK)
    )
    key_rows = (
        jnp.dot(tokens, w_key, preferred_element_type=jnp.float32)
        .astype(jnp.bfloat16)
        .reshape(row_count, local_heads, DK)
    )
    value_matrix = (
        jnp.dot(tokens, value_weight, preferred_element_type=jnp.float32)
        .astype(jnp.bfloat16)
        .reshape(row_count, local_heads, DV)
    )
    block_state = jnp.einsum(
        "hfn,nhd->hfd", key_features(key_rows), value_matrix, preferred_element_type=jnp.float32
    )
    zero_state = jnp.zeros(block_state.shape, jnp.float32)
    my_block = lax.axis_index("seq")
    piece = lax.all_gather(
        block_state[None].astype(jnp.bfloat16), "seq", axis=0, tiled=True
    ).astype(jnp.float32)
    order = lax.broadcasted_iota(jnp.int32, (piece.shape[0],), 0)
    keep = (order < my_block).astype(jnp.float32)
    earlier = zero_state + jnp.sum(piece * keep[:, None, None, None], axis=0)
    scores = (
        jnp.einsum("nha,mha->hnm", query_rows, key_rows, preferred_element_type=jnp.float32) * 0.25
    )
    causal = lax.broadcasted_iota(jnp.int32, (row_count, row_count), 0) >= lax.broadcasted_iota(
        jnp.int32, (row_count, row_count), 1
    )
    weight_tensors = jnp.where(causal[None], 1.0 + scores + 0.5 * scores * scores, 0.0).astype(
        jnp.bfloat16
    )
    local_portion = jnp.einsum(
        "iot,tiw->oiw", weight_tensors, value_matrix, preferred_element_type=jnp.float32
    )
    carried = jnp.einsum("hfn,hfd->nhd", query_features(query_rows), earlier)
    numerator = carried + local_portion
    scale = lax.rsqrt(jnp.mean(numerator * numerator, axis=-1, keepdims=True) + 1e-06)
    normalized_rows = (numerator * scale).reshape(row_count, local_heads * DV).astype(jnp.bfloat16)
    mixed = jnp.dot(
        lax.all_gather(normalized_rows, "feat", axis=1, tiled=True),
        w_out,
        preferred_element_type=jnp.float32,
    )
    return mixed.astype(jnp.bfloat16)


def solution(mesh):
    placed = (
        P(("dp", "seq"), None),
        P(None, "feat"),
        P(None, "feat"),
        P(None, "feat"),
        P(None, "feat"),
    )
    return jax.shard_map(
        local, mesh=mesh, in_specs=placed, out_specs=P(("dp", "seq"), "feat"), check_vma=False
    )
```

profile of v0, /device:TPU:1, one launch (start us, length us, event | category | flops | bytes accessed | tf_op | source)
XLA Modules:
  0.0 145.9 jit_solution(15767206818004288337)
XLA Ops:
  6.5 0.0 copy-start
  6.5 0.0 all-gather.6.cloned.1.call-start
  6.5 0.0 copy-start.1
  6.5 3.7 %convolution_convert_fusion.4 = bf16[1024,32]{0,1:T(8,128)(2,1)S(1)} fusion(bf16[1024,2048]{1,0:T(8,128)(2,1)} %param.5, bf16[2048,32]{0,1:T(8,128)(2,1)} %param.7), kind=kOutput, calls=%fused_computation.25 | convolution fusion | flops 134250496 | bytes 4390912 | tf_op jit(solution)/shard_map/dot_general | solution.py:41
  10.2 0.0 copy-done
  10.3 0.1 copy-done.1
  10.3 1.3 convolution_convert_fusion.1
  11.6 0.0 copy-start.4
  11.7 0.0 copy-start.2
  11.7 0.2 multiply_convert_fusion
  11.9 0.6 copy-done.4
  12.4 1.2 convolution_convert_fusion.2
  13.6 0.0 all-gather.6.cloned.1.call-update
  13.7 0.0 all-gather.4.cloned.1.call-start
  13.8 0.3 iota_compare_fusion
  14.1 0.0 copy-done.2
  14.1 3.5 %convolution_convert_fusion.3 = bf16[1024,32]{0,1:T(8,128)(2,1)S(1)} fusion(bf16[1024,2048]{1,0:T(8,128)(2,1)} %param.5, bf16[2048,32]{0,1:T(8,128)(2,1)S(1)} %copy-done.2), kind=kOutput, calls=%fused_computation.24 | convolution fusion | flops 134250496 | bytes 4390912 | tf_op jit(solution)/shard_map/dot_general | solution.py:36
  17.6 0.2 multiply_multiply_fusion
  17.8 5.4 %fusion.1 = f32[2,128,1024]{2,1,0:T(8,128)} fusion(bf16[1024,2,128]{0,2,1:T(8,128)(2,1)} %bitcast.47, pred[1024,1024]{1,0:T(8,128)(4,1)S(1)} %iota_compare_fusion, bf16[1024,2,16]{0,2,1:T(8,128)(2,1)S(1)} %bitcast.45, bf16[1024,2,16]{0,2,1:T(8,128)(2,1)S(1)} %bitcast.43), kind=kOutput, calls=%fused_computation.4 | convolution fusion | flops 618659840 | bytes 2752512 | tf_op jit(solution)/shard_map/iot,tiw->oiw/dot_general | solution.py:70
  23.2 0.0 copy-start.3
  23.2 59.8 %all-gather.6.cloned.1.call-done = bf16[32,273,128]{2,1,0:T(8,128)(2,1)} async-done(((bf16[2,273,128]{2,1,0:T(8,128)(2,1)}), bf16[32,273,128]{2,1,0:T(8,128)(2,1)}) %all-gather.6.cloned.1.call-update) | async-done | bytes 2236432 | tf_op jit(solution)/shard_map/all_gather | solution.py:55
  83.0 2.2 %fusion = bf16[2,273,128]{2,1,0:T(8,128)(2,1)S(1)} fusion(bf16[16,2,273,128]{3,2,1,0:T(8,128)(2,1)} %bitcast.37, f32[16]{0:T(128)S(1)} %compare_convert_fusion), kind=kLoop, calls=%fused_computation.2 | loop fusion | flops 3284736 | bytes 2376256 | tf_op jit(solution)/shard_map/reduce_sum | solution.py:60
  85.2 1.9 %multiply_reduce_fusion = (f32[1024,2]{0,1:T(2,128)S(1)}, f32[1024,2,128]{0,2,1:T(8,128)S(1)}) fusion(f32[2,128,1024]{2,1,0:T(8,128)} %fusion.1, bf16[2,273,128]{2,1,0:T(8,128)(2,1)S(1)} %fusion, bf16[2,256,1024]{2,1,0:T(8,128)(2,1)S(1)} %bitcast.39, bf16[2,16,1024]{2,1,0:T(8,128)(2,1)S(1)} %get-tuple-element.5, bf16[273]{0:T(512)(128)(2,1)S(1)} %pad.clone), kind=kOutput, calls=%fused_computation.27 | convolution fusion | flops 147269632 | bytes 3359778 | tf_op jit(solution)/shard_map/hfn,hfd->nhd/dot_general | solution.py:73
  87.1 0.9 multiply_convert_fusion.1
  88.0 0.0 all-gather.4.cloned.1.call-update
  88.0 46.7 %all-gather.4.cloned.1.call-done = bf16[1024,2048]{0,1:T(8,128)(2,1)} async-done(((bf16[1024,256]{0,1:T(8,128)(2,1)}), bf16[1024,2048]{0,1:T(8,128)(2,1)}) %all-gather.4.cloned.1.call-update) | async-done | bytes 4194320 | tf_op jit(solution)/shard_map/all_gather | solution.py:78
  134.8 0.0 copy-done.3
  134.8 4.3 %convolution_convert_fusion = bf16[1024,256]{1,0:T(8,128)(2,1)} fusion(bf16[1024,2048]{0,1:T(8,128)(2,1)} %all-gather.4.cloned.1.call-done, bf16[2048,256]{1,0:T(8,128)(2,1)S(1)} %copy-done.3), kind=kOutput, calls=%fused_computation.16 | convolution fusion | flops 1074003968 | bytes 5767168 | tf_op jit(solution)/shard_map/dot_general | solution.py:77
  (6 shorter events, 0.1 us)
Async XLA Ops:
  6.5 3.7 %copy-start = (bf16[2048,256]{1,0:T(8,128)(2,1)S(1)}, bf16[2048,256]{1,0:T(8,128)(2,1)}, u32[]{:S(2)}) copy-start(bf16[2048,256]{1,0:T(8,128)(2,1)} %param.8) | copy-start | bytes 3145732
  6.5 76.5 %all-gather.6.cloned.1.call-start = ((), (), s32[]{:S(2)}) async-start(), calls=%async_computation.1 | async-start | bytes 2437120 | tf_op jit(solution)/shard_map/all_gather | solution.py:55
  6.5 3.8 %copy-start.1 = (bf16[1024,2048]{1,0:T(8,128)(2,1)S(1)}, bf16[1024,2048]{1,0:T(8,128)(2,1)}, u32[]{:S(2)}) copy-start(bf16[1024,2048]{1,0:T(8,128)(2,1)} %param.5) | copy-start | bytes 12582916
  11.6 0.8 copy-start.4
  11.7 2.4 %copy-start.2 = (bf16[2048,32]{0,1:T(8,128)(2,1)S(1)}, bf16[2048,32]{0,1:T(8,128)(2,1)}, u32[]{:S(2)}) copy-start(bf16[2048,32]{0,1:T(8,128)(2,1)} %param.6) | copy-start | bytes 393220
  13.7 121.1 %all-gather.4.cloned.1.call-start = ((), (), s32[]{:S(2)}) async-start(), calls=%async_computation | async-start | bytes 4718592 | tf_op jit(solution)/shard_map/all_gather | solution.py:78
  23.2 111.5 %copy-start.3 = (bf16[2048,256]{1,0:T(8,128)(2,1)S(1)}, bf16[2048,256]{1,0:T(8,128)(2,1)}, u32[]{:S(2)}) copy-start(bf16[2048,256]{1,0:T(8,128)(2,1)} %param.9) | copy-start | bytes 3145732
Sparse Core Ops, SparseCore 0:
  13.8 69.1 all-gather.5
  88.2 46.5 all-gather.3
where the time goes:
time: 146 us
  waiting for transfers between devices  107 us (73%)
  matrix products  21.3 us (15%)
  between operations  13.5 us (9%)
  other arithmetic  3.82 us (3%)
    all_gather x1, waiting for transfers between devices, local(): lax.all_gather(block_state[None].astype(jnp.bfloat16), 'seq', axis=0, til...  59.8 us
    all_gather x1, waiting for transfers between devices, local(): lax.all_gather(normalized_rows, 'feat', axis=1, tiled=True)  46.7 us
    dot_general x1, matrix products, local(): jnp.einsum('iot,tiw->oiw', weight_tensors, value_matrix, preferred_elemen...  5.39 us
    dot_general x1, matrix products, local(): jnp.dot(lax.all_gather(normalized_rows, 'feat', axis=1, tiled=True), w_ou...  4.32 us
    dot_general x1, matrix products, local(): jnp.dot(tokens, w_key, preferred_element_type=jnp.float32)  3.67 us
    dot_general x1, matrix products, local(): jnp.dot(tokens, w_query, preferred_element_type=jnp.float32)  3.52 us
  transfers between devices with their start and end apart: 2, of which 2 were waited for; matrix products, arithmetic and copies ran while one was open for 6% of the time, Pallas kernels for 0%

commit v1 on v0

v1 whole, which is shorter than its diff:
```python
import functools

import jax
import jax.numpy as jnp
import numpy as np
from jax import lax
from jax.experimental import pallas as pl
from jax.experimental.pallas import tpu as pltpu
from jax.sharding import PartitionSpec as P

DK = 16
DV = 128
FEATS = 160
LANES = 128
ONE = 64
CHUNK = 16
CHUNKS = FEATS // CHUNK
MESH = pl.DeviceIdType.MESH


def selectors(first, ones_at, width, query):
    left = np.zeros((2 * FEATS, width), np.float32)
    right = np.zeros((2 * FEATS, width), np.float32)
    for head in range(2):
        row = head * FEATS
        base = first + head * DK
        left[row, ones_at] = 2.0 if query else 1.0
        right[row, ones_at] = 1.0
        row += 1
        for a in range(DK):
            left[row, base + a] = 0.5 if query else 1.0
            right[row, ones_at] = 1.0
            row += 1
        for a in range(DK):
            for b in range(a, DK):
                left[row, base + a] = (0.0625 if a == b else 0.125) if query else 1.0
                right[row, base + b] = 1.0
                row += 1
    return left, right


def remote(src, dst, send, recv, device):
    return pltpu.make_async_remote_copy(
        src_ref=src, dst_ref=dst, send_sem=send, recv_sem=recv, device_id=device, device_id_type=MESH
    )


def kernel(
    n_seq, tok, wq, wk, wv, wo, e1k, e2k, e1q, e2q, out,
    tok_v, wq_v, wk_v, wv_v, wqk_v, wo_v, e1k_v, e2k_v, e1q_v, e2q_v,
    qk_v, qkt, kaug, v_v, state, st, p1, p2, qx, phi, sx, lown, lx, acc_own, acc_oth, outp,
    load_sem, p1_send, p1_recv, p2_send, p2_recv, q_send, q_recv, w_send, w_recv,
    l_send, l_relay, l_recv, s_send, s_recv, o_send, o_recv,
):
    f32, bf16 = jnp.float32, jnp.bfloat16
    rows = tok.shape[0]
    rb = rows // 4
    half = rows // 2
    z = lax.axis_index("seq")
    f = lax.axis_index("feat")
    y = f // 2
    core = f % 2
    other = 1 - core
    yr, yl, yo = (y + 1) % 4, (y + 3) % 4, (y + 2) % 4
    partner = 2 * y + other

    barrier = pltpu.get_barrier_semaphore()
    for off in range(1, n_seq):
        pl.semaphore_signal(barrier, inc=1, device_id={"seq": (z + off) % n_seq}, device_id_type=MESH)
    for off in range(1, 8):
        pl.semaphore_signal(barrier, inc=1, device_id={"feat": (f + off) % 8}, device_id_type=MESH)

    def load(src, dst, k):
        return pltpu.make_async_copy(src, dst, load_sem.at[k])

    loads = [
        load(wq, wq_v, 0), load(wk, wk_v, 1), load(wv, wv_v, 2),
        *[load(tok.at[pl.ds(r * rb, rb)], tok_v.at[pl.ds(r * rb, rb)], 3 + r) for r in range(4)],
        load(e1k, e1k_v, 7), load(e2k, e2k_v, 8), load(e1q, e1q_v, 9), load(e2q, e2q_v, 10),
    ]
    own_w = load(wo, wo_v.at[core], 11)
    for copy in loads:
        copy.start()
    own_w.start()

    kaug[...] = jnp.zeros_like(kaug)
    one_row = (lax.broadcasted_iota(jnp.int32, (1, LANES), 1) == ONE).astype(f32)
    for k in range(8):
        qx[k, pl.ds(2 * DK, DK), :] = (
            lax.broadcasted_iota(jnp.int32, (DK, half), 0) == 0
        ).astype(f32).astype(bf16)
    loads[0].wait()
    loads[1].wait()
    wqk_v[...] = jnp.transpose(jnp.concatenate(
        [wq_v[...], wk_v[...], jnp.zeros((LANES - 4 * DK, wq_v.shape[1]), bf16)], axis=0
    ).astype(f32)).astype(bf16)
    loads[2].wait()
    for k in range(7, 11):
        if k == 7:
            loads[3].wait()
        loads[k].wait()

    for r in range(4):
        if r:
            loads[3 + r].wait()
        span = pl.ds(r * rb, rb)
        x = tok_v[span, :]
        qk = jnp.dot(x, wqk_v[...], preferred_element_type=f32) + one_row
        qk = qk.astype(bf16)
        qk_v[span, :] = qk
        turned = jnp.transpose(qk.astype(f32)).astype(bf16)
        qkt[:, span] = turned
        value = jnp.dot(x, wv_v[...], preferred_element_type=f32).astype(bf16)
        v_v[span, :] = value
        features = (
            jnp.dot(e1k_v[...], turned, preferred_element_type=f32)
            * jnp.dot(e2k_v[...], turned, preferred_element_type=f32)
        ).astype(bf16)
        for h in range(2):
            term = jnp.dot(
                features[h * FEATS:(h + 1) * FEATS], value[:, h * DV:(h + 1) * DV], preferred_element_type=f32
            )
            lanes = pl.ds(h * DV, DV)
            if r == 0:
                state[:, lanes] = term
            elif r < 3:
                state[:, lanes] += term
            else:
                st[:, lanes] = (state[:, lanes] + term).astype(bf16)

    pl.semaphore_wait(barrier, n_seq - 1 + 7)

    def owner_of(k):
        return (k * n_seq) // CHUNKS

    def chunk_of(device):
        k = (CHUNKS * device + n_seq - 1) // n_seq
        return jnp.minimum(k, CHUNKS - 1), (k < CHUNKS) & (owner_of(k) == device)

    my_chunk, is_owner = chunk_of(z)
    offsets = sorted(range(1, n_seq), key=lambda o: -min(o, n_seq - o))

    def to_owner(k, target):
        chunk, _ = chunk_of(target)
        return remote(
            st.at[pl.ds(pl.multiple_of(chunk * CHUNK, CHUNK), CHUNK)], p1.at[z],
            p1_send.at[k], p1_recv.at[z], {"seq": target},
        )

    for k, off in enumerate(offsets):
        target = (z + off) % n_seq

        @pl.when(chunk_of(target)[1])
        def _():
            to_owner(k, target).start()

    @pl.when(is_owner)
    def _():
        p1[z] = st[pl.ds(pl.multiple_of(my_chunk * CHUNK, CHUNK), CHUNK), :]

    q_copies = []
    for j in range(2):
        lanes = pl.ds(j * half, half)
        for k, yy in enumerate((yr, yl, yo)):
            q_copies.append(remote(
                qkt.at[pl.ds(0, 2 * DK), lanes], qx.at[f, pl.ds(0, 2 * DK)],
                q_send.at[j * 3 + k], q_recv.at[f], {"feat": 2 * yy + j},
            ))
    q_copies.append(remote(
        qkt.at[pl.ds(0, 2 * DK), pl.ds(pl.multiple_of(other * half, half), half)],
        qx.at[f, pl.ds(0, 2 * DK)], q_send.at[6], q_recv.at[f], {"feat": partner},
    ))
    for copy in q_copies:
        copy.start()
    qx[f, pl.ds(0, 2 * DK), :] = qkt[pl.ds(0, 2 * DK), pl.ds(pl.multiple_of(core * half, half), half)]

    own_w.wait()
    w_copy = remote(wo_v.at[core], wo_v.at[core], w_send, w_recv, {"feat": partner})
    w_copy.start()

    for h in range(2):
        kaug[h, pl.ds(h * DK, DK), :] = (
            qkt[pl.ds((2 + h) * DK, DK), :].astype(f32) * 0.25
        ).astype(bf16)
        kaug[h, pl.ds(ONE, DK), :] = qkt[pl.ds(ONE, DK), :]
    causal = lax.broadcasted_iota(jnp.int32, (rb, rb), 0) >= lax.broadcasted_iota(jnp.int32, (rb, rb), 1)
    l_copies = []
    for r in range(4):
        span = pl.ds(r * rb, rb)
        j, b = r // 2, r % 2
        for h in range(2):
            lanes = pl.ds(h * DV, DV)
            raised = jnp.dot(
                qk_v[span, :], kaug[h, :, pl.ds(r * rb, rb)], preferred_element_type=f32
            )
            weight = jnp.where(causal, raised * raised + 1.0, 0.0).astype(bf16)
            total = jnp.dot(weight, v_v[span, lanes], preferred_element_type=f32)
            if r:
                raised = jnp.dot(
                    qk_v[span, :], kaug[h, :, pl.ds(0, r * rb)], preferred_element_type=f32
                )
                weight = (raised * raised + 1.0).astype(bf16)
                total += jnp.dot(weight, v_v[pl.ds(0, r * rb), lanes], preferred_element_type=f32)
            lown[span, lanes] = total.astype(bf16)

        for k, yy in enumerate((yr, yl)):
            copy = remote(
                lown.at[span], lx.at[f, pl.ds(b * rb, rb)], l_send.at[r, k], l_recv.at[f, b],
                {"feat": 2 * yy + j},
            )
            copy.start()
            l_copies.append(copy)
        across = remote(
            lown.at[span], lx.at[f, pl.ds(b * rb, rb)], l_send.at[r, 2], l_recv.at[f, b],
            {"feat": partner},
        )

        @pl.when(core != j)
        def _():
            across.start()

        @pl.when(core == j)
        def _():
            lx[f, pl.ds(b * rb, rb), :] = lown[span, :]

    def make_phi(g, _):
        source = (f + g) % 8

        @pl.when(g > 0)
        def _():
            remote(
                qkt.at[pl.ds(0, 2 * DK), pl.ds(0, half)], qx.at[source, pl.ds(0, 2 * DK)],
                q_send.at[0], q_recv.at[source], {"feat": partner},
            ).wait_recv()

        q = qx[source]
        turned = (
            jnp.dot(e1q_v[...], q, preferred_element_type=f32)
            * jnp.dot(e2q_v[...], q, preferred_element_type=f32)
        )
        for h in range(2):
            phi[source, h] = jnp.transpose(turned[h * FEATS:(h + 1) * FEATS]).astype(bf16)
        return 0

    lax.fori_loop(0, 8, make_phi, 0)

    def back(k, target):
        return remote(
            p2.at[target], sx.at[f, pl.ds(pl.multiple_of(my_chunk * CHUNK, CHUNK), CHUNK)],
            p2_send.at[k], p2_recv.at[my_chunk], {"seq": target},
        )

    @pl.when(is_owner)
    def _():
        def arrive(s, _):
            @pl.when(s != z)
            def _():
                remote(
                    st.at[pl.ds(0, CHUNK)], p1.at[s], p1_send.at[0], p1_recv.at[s], {"seq": s}
                ).wait_recv()
            return 0

        lax.fori_loop(0, n_seq, arrive, 0)
        total = jnp.zeros((CHUNK, 2 * DV), f32)
        for c in range(n_seq):
            p2[c] = total.astype(bf16)
            total = total + p1[c].astype(f32)
        for k, off in enumerate(offsets):
            back(k, (z + off) % n_seq).start()
        sx[f, pl.ds(pl.multiple_of(my_chunk * CHUNK, CHUNK), CHUNK), :] = p2[z]

    def l_wait(source, b):
        remote(
            lown.at[pl.ds(0, rb)], lx.at[source, pl.ds(b * rb, rb)], l_send.at[0, 0],
            l_recv.at[source, b], {"feat": partner},
        ).wait_recv()

    relays = []
    for b in range(2):
        for k, (source, to) in enumerate(((2 * yl, yr), (2 * yr + 1, yl))):
            l_wait(source, b)
            copy = remote(
                lx.at[source, pl.ds(b * rb, rb)], lx.at[source, pl.ds(b * rb, rb)],
                l_relay.at[k, b], l_recv.at[source, b], {"feat": 2 * to + core},
            )
            copy.start()
            relays.append(copy)

    def chunk_in(k, _):
        @pl.when(owner_of(k) != z)
        def _():
            remote(
                p2.at[0], sx.at[f, pl.ds(pl.multiple_of(k * CHUNK, CHUNK), CHUNK)],
                p2_send.at[0], p2_recv.at[k], {"seq": 0},
            ).wait_recv()
        return 0

    lax.fori_loop(0, CHUNKS, chunk_in, 0)

    def s_copy(k, source, target):
        return remote(sx.at[source], sx.at[source], s_send.at[k], s_recv.at[source], {"feat": target})

    def s_wait(source):
        s_copy(0, source, partner).wait_recv()

    near = (2 * yr + core, 2 * yl + core, 2 * yo + core)
    s_copies = [s_copy(k, f, target) for k, target in enumerate((near[2], near[0], near[1], partner))]
    for copy in s_copies:
        copy.start()

    w_copy.wait_recv()

    def finish(source, first=False):
        for h in range(2):
            lanes = pl.ds(h * DV, DV)
            number = jnp.dot(
                phi[source, h], sx[source, :, lanes], preferred_element_type=f32
            ) + lx[source, :, lanes].astype(f32)
            scale = lax.rsqrt(jnp.mean(number * number, axis=-1, keepdims=True) + 4e-6)
            lown[pl.ds(0, half), lanes] = (number * scale).astype(bf16)
        normed = lown[pl.ds(0, half), :]
        deep = pl.ds(pl.multiple_of(source * 2 * DV, 2 * DV), 2 * DV)
        for acc, which in ((acc_oth, other), (acc_own, core)):
            term = jnp.dot(normed, wo_v[which, deep, :], preferred_element_type=f32)
            if first:
                acc[...] = term
            else:
                acc[...] += term

    for copy in l_copies:
        copy.wait_send()
    for r in range(4):
        @pl.when(core != r // 2)
        def _():
            remote(
                lown.at[pl.ds(r * rb, rb)], lx.at[f, pl.ds((r % 2) * rb, rb)], l_send.at[r, 2],
                l_recv.at[f, r % 2], {"feat": partner},
            ).wait_send()

    finish(f, first=True)
    s_wait(partner)
    for b in range(2):
        l_wait(partner, b)
    finish(partner)
    passed = []
    for k, source in enumerate(near):
        s_wait(source)
        copy = s_copy(4 + k, source, partner)
        copy.start()
        passed.append(copy)
    for k, yy in enumerate((yr, yl, yo)):
        source = 2 * yy + core
        for b in range(2):
            if k == 0:
                @pl.when(core == 0)
                def _():
                    l_wait(source, b)
            elif k == 1:
                @pl.when(core == 1)
                def _():
                    l_wait(source, b)
            else:
                l_wait(source, b)
        finish(source)
    for k, yy in enumerate((yr, yl, yo)):
        source = 2 * yy + other
        s_wait(source)
        for b in range(2):
            if k == 0:
                @pl.when(other == 0)
                def _():
                    l_wait(source, b)
            elif k == 1:
                @pl.when(other == 1)
                def _():
                    l_wait(source, b)
            else:
                l_wait(source, b)
        finish(source)

    mine = pl.ds(pl.multiple_of(core * half, half), half)
    outp[...] = acc_oth[...].astype(bf16)
    out_copy = remote(outp, out.at[mine], o_send, o_recv, {"feat": partner})
    out_copy.start()
    out[mine, :] = acc_own[...].astype(bf16)

    for k, off in enumerate(offsets):
        target = (z + off) % n_seq

        @pl.when(chunk_of(target)[1])
        def _():
            to_owner(k, target).wait_send()

    @pl.when(is_owner)
    def _():
        for k, off in enumerate(offsets):
            back(k, (z + off) % n_seq).wait_send()

    for copy in q_copies + [w_copy] + relays + s_copies + passed:
        copy.wait_send()
    out_copy.wait_send()
    remote(
        outp, out.at[pl.ds(pl.multiple_of(other * half, half), half)], o_send, o_recv, {"feat": partner}
    ).wait_recv()


def local(n_seq, consts, tokens, w_query, w_key, value_weight, w_out):
    rows, deep = tokens.shape
    cols = value_weight.shape[1]
    half = rows // 2
    f32, bf16 = jnp.float32, jnp.bfloat16
    dma = pltpu.SemaphoreType.DMA
    anywhere = pl.BlockSpec(memory_space=pl.ANY)
    vm = pltpu.VMEM
    width = w_query.shape[1]
    return pl.pallas_call(
        functools.partial(kernel, n_seq),
        out_shape=jax.ShapeDtypeStruct((rows, cols), bf16),
        in_specs=[anywhere] * 9,
        out_specs=pl.BlockSpec(memory_space=pltpu.VMEM),
        scratch_shapes=[
            vm((rows, deep), bf16), vm((width, deep), bf16), vm((width, deep), bf16),
            vm((deep, cols), bf16), vm((deep, LANES), bf16), vm((2, 8 * cols, cols), bf16),
            vm((2 * FEATS, LANES), bf16), vm((2 * FEATS, LANES), bf16),
            vm((2 * FEATS, 3 * DK), bf16), vm((2 * FEATS, 3 * DK), bf16),
            vm((rows, LANES), bf16), vm((LANES, rows), bf16), vm((2, LANES, rows), bf16),
            vm((rows, cols), bf16), vm((FEATS, cols), f32), vm((FEATS, cols), bf16),
            vm((n_seq, CHUNK, cols), bf16), vm((n_seq, CHUNK, cols), bf16),
            vm((8, 3 * DK, half), bf16), vm((8, 2, half, FEATS), bf16), vm((8, FEATS, cols), bf16),
            vm((rows, cols), bf16), vm((8, half, cols), bf16),
            vm((half, cols), f32), vm((half, cols), f32), vm((half, cols), bf16),
            dma((12,)), dma((n_seq,)), dma((n_seq,)), dma((n_seq,)), dma((CHUNKS,)),
            dma((7,)), dma((8,)), dma, dma,
            dma((4, 3)), dma((2, 2)), dma((8, 2)), dma((7,)), dma((8,)), dma, dma,
        ],
        compiler_params=pltpu.CompilerParams(
            collective_id=0, has_side_effects=True, vmem_limit_bytes=56 * 1024 * 1024
        ),
    )(tokens, w_query.T, w_key.T, value_weight, w_out, *consts)


def solution(mesh):
    consts = [
        jnp.asarray(e, jnp.bfloat16)
        for e in (*selectors(2 * DK, ONE, LANES, False), *selectors(0, 2 * DK, 3 * DK, True))
    ]
    placed = (P(("dp", "seq"), None),) + (P(None, "feat"),) * 4

    def run(*args):
        return jax.shard_map(
            functools.partial(local, mesh.shape["seq"], consts),
            mesh=mesh, in_specs=placed, out_specs=P(("dp", "seq"), "feat"), check_vma=False,
        )(*args)

    return run
```

time: 146 us -> 50.5 us (0.35)
  waiting for transfers between devices: 107 us -> 0 us
  Pallas kernels: 0 us -> 48.5 us
  matrix products: 21.3 us -> 0 us
  between operations: 13.5 us -> 0.01 us
  other arithmetic: 3.82 us -> 0 us
    all_gather x2 -> x0, waiting for transfers between devices: 107 us -> none  [the longest x1 59.8 us: local(): lax.all_gather(block_state[None].astype(jnp.bfloat16), 'seq', axis=0, til...]
    pallas_call x0 -> x1, Pallas kernels: none -> 48.5 us  [local(): pl.pallas_call(functools.partial(kernel, n_seq), out_shape=jax.ShapeDtype...]
    dot_general x7 -> x0, matrix products: 21.3 us -> none  [the longest x1 5.39 us: local(): jnp.einsum('iot,tiw->oiw', weight_tensors, value_matrix, preferred_elemen...]
    reduce_sum x1 -> x0, other arithmetic: 2.17 us -> none  [local(): earlier = zero_state + jnp.sum(piece * keep[:, None, None, None], axis=0)]
  transfers between devices with their start and end apart: 2 -> 0, of which waited for: 2 -> 0; matrix products, arithmetic and copies ran while one was open for 6% -> 0% of each run, Pallas kernels for 0% -> 0%
where the time goes in v1:
time: 50.5 us; the launch traced here: 50.4 us
  Pallas kernels  48.5 us (96%)
  local copies, waits for them, and re-layouts  1.87 us (4%)
    pallas_call x1, Pallas kernels, local(): pl.pallas_call(functools.partial(kernel, n_seq), out_shape=jax.ShapeDtype...  48.5 us
    unnamed x1, local copies, waits for them, and re-layouts  1.87 us

profile of v1, /device:TPU:1, one launch (start us, length us, event | category | flops | bytes accessed | tf_op | source)
XLA Modules:
  0.0 50.4 jit_solution(4003658367374544988)
XLA Ops:
  0.0 48.5 %shard_map.91 = bf16[1024,256]{1,0:T(8,128)(2,1)} custom-call(bf16[1024,2048]{1,0:T(8,128)(2,1)} %tok.1, bf16[32,2048]{1,0:T(8,128)(2,1)} %bitcast.2, bf16[32,2048]{1,0:T(8,128)(2,1)} %bitcast.3, bf16[2048,256]{1,0:T(8,128)(2,1)} %wv.1, bf16[2048,256]{1,0:T(8,128)(2,1)} %wo.1, bf16[320,128]{1,0:T(8,128)(2,1)} %constant.8.clone.e1k, ...), custom_call_target="tpu_custom_call" | custom-call | tf_op jit(solution)/shard_map/pallas_call | solution.py:416
  48.5 1.9 %copy.11 = bf16[1024,256]{1,0:T(8,128)(2,1)} copy(bf16[1024,256]{1,0:T(8,128)(2,1)} %shard_map.91) | data formatting | bytes 1048576

commit v2 on v1

v2 whole, which is shorter than its diff:
```python
import functools

import jax
import jax.numpy as jnp
import numpy as np
from jax import lax
from jax.experimental import pallas as pl
from jax.experimental.pallas import tpu as pltpu
from jax.sharding import PartitionSpec as P

DK = 16
DV = 128
FEATS = 160
LANES = 128
ONE = 64
CHUNK = 16
CHUNKS = FEATS // CHUNK
LOW = 3
MESH = pl.DeviceIdType.MESH


def selectors(first, ones_at, width, query):
    left = np.zeros((2 * FEATS, width), np.float32)
    right = np.zeros((2 * FEATS, width), np.float32)
    for head in range(2):
        row = head * FEATS
        base = first + head * DK
        left[row, ones_at] = 2.0 if query else 1.0
        right[row, ones_at] = 1.0
        row += 1
        for a in range(DK):
            left[row, base + a] = 0.5 if query else 1.0
            right[row, ones_at] = 1.0
            row += 1
        for a in range(DK):
            for b in range(a, DK):
                left[row, base + a] = (0.0625 if a == b else 0.125) if query else 1.0
                right[row, base + b] = 1.0
                row += 1
    return left, right


def remote(src, dst, send, recv, device):
    return pltpu.make_async_remote_copy(
        src_ref=src, dst_ref=dst, send_sem=send, recv_sem=recv, device_id=device, device_id_type=MESH
    )


def kernel(
    n_seq, tok, wq, wk, wv, wo, e1k, e2k, e1q, e2q, out,
    tok_v, wq_v, wk_v, wv_v, wqk_v, wo_v, e1k_v, e2k_v, e1q_v, e2q_v,
    qk_v, qkt, kaug, v_v, state, st, p1, p2, qx, phi, sx, early, lown, lx, nrm, acc, outp,
    load_sem, p1_send, p1_recv, e_recv, p2_send, p2_recv, q_send, q_recv, w_send, w_recv,
    l_send, l_relay, l_recv, s_send, s_recv, o_send, o_recv,
):
    f32, bf16 = jnp.float32, jnp.bfloat16
    rows = tok.shape[0]
    rb = rows // 4
    half = rows // 2
    z = lax.axis_index("seq")
    f = lax.axis_index("feat")
    y = f // 2
    core = f % 2
    other = 1 - core
    yr, yl, yo = (y + 1) % 4, (y + 3) % 4, (y + 2) % 4
    partner = 2 * y + other

    def signal(sem, **device):
        pl.semaphore_signal(sem, inc=1, device_id=device, device_id_type=MESH)

    barrier = pltpu.get_barrier_semaphore()
    for off in range(1, 8):
        signal(barrier, feat=(f + off) % 8)
    first_owner = LOW + 1
    is_low = z <= LOW
    is_last_low = z == LOW
    owns = (z >= first_owner) & (z < first_owner + CHUNKS)
    for t in range(LOW + 1):
        @pl.when(is_low & (z != t))
        def _():
            signal(barrier, seq=t)

    @pl.when(owns)
    def _():
        signal(barrier, seq=LOW)

    for t in range(first_owner, n_seq):
        @pl.when((z > LOW) & (z != t))
        def _():
            signal(barrier, seq=t)

    greetings = 7 + jnp.where(is_low, LOW, n_seq - 2 - LOW) + jnp.where(is_last_low, CHUNKS, 0)

    def load(src, dst, k):
        return pltpu.make_async_copy(src, dst, load_sem.at[k])

    w_loads = [load(wq, wq_v, 0), load(wk, wk_v, 1)]
    v_load = load(wv, wv_v, 2)
    t_loads = [load(tok.at[pl.ds(r * rb, rb)], tok_v.at[pl.ds(r * rb, rb)], 3 + r) for r in range(4)]
    k_loads = [load(e1k, e1k_v, 7), load(e2k, e2k_v, 8)]
    q_loads = [load(e1q, e1q_v, 9), load(e2q, e2q_v, 10)]
    own_w = load(wo, wo_v.at[core], 11)
    for copy in (*w_loads, v_load, t_loads[0], *k_loads, *t_loads[1:], *q_loads, own_w):
        copy.start()

    kaug[...] = jnp.zeros_like(kaug)
    one_row = (lax.broadcasted_iota(jnp.int32, (1, LANES), 1) == ONE).astype(f32)
    for k in range(8):
        qx[k, pl.ds(2 * DK, DK), :] = (
            lax.broadcasted_iota(jnp.int32, (DK, half), 0) == 0
        ).astype(f32).astype(bf16)
    for copy in w_loads:
        copy.wait()
    wqk_v[...] = jnp.transpose(jnp.concatenate(
        [wq_v[...], wk_v[...], jnp.zeros((LANES - 4 * DK, wq_v.shape[1]), bf16)], axis=0
    ).astype(f32)).astype(bf16)
    v_load.wait()

    causal = lax.broadcasted_iota(jnp.int32, (rb, rb), 0) >= lax.broadcasted_iota(jnp.int32, (rb, rb), 1)

    def project(r):
        span = pl.ds(r * rb, rb)
        x = tok_v[span, :]
        qk = (jnp.dot(x, wqk_v[...], preferred_element_type=f32) + one_row).astype(bf16)
        qk_v[span, :] = qk
        turned = jnp.transpose(qk.astype(f32)).astype(bf16)
        qkt[:, span] = turned
        for h in range(2):
            kaug[h, pl.ds(h * DK, DK), span] = (
                turned[(2 + h) * DK:(3 + h) * DK].astype(f32) * 0.25
            ).astype(bf16)
            kaug[h, pl.ds(ONE, DK), span] = turned[ONE:ONE + DK]
        v_v[span, :] = jnp.dot(x, wv_v[...], preferred_element_type=f32).astype(bf16)

    def add_state(r):
        span = pl.ds(r * rb, rb)
        turned = qkt[:, span]
        features = (
            jnp.dot(e1k_v[...], turned, preferred_element_type=f32)
            * jnp.dot(e2k_v[...], turned, preferred_element_type=f32)
        ).astype(bf16)
        for h in range(2):
            lanes = pl.ds(h * DV, DV)
            term = jnp.dot(features[h * FEATS:(h + 1) * FEATS], v_v[span, lanes], preferred_element_type=f32)
            if r == 0:
                state[:, lanes] = term
            elif r < 3:
                state[:, lanes] += term
            else:
                st[:, lanes] = (state[:, lanes] + term).astype(bf16)

    def own_portion(r):
        span = pl.ds(r * rb, rb)
        for h in range(2):
            lanes = pl.ds(h * DV, DV)
            raised = jnp.dot(qk_v[span, :], kaug[h, :, span], preferred_element_type=f32)
            weight = jnp.where(causal, raised * raised + 1.0, 0.0).astype(bf16)
            total = jnp.dot(weight, v_v[span, lanes], preferred_element_type=f32)
            if r:
                raised = jnp.dot(qk_v[span, :], kaug[h, :, pl.ds(0, r * rb)], preferred_element_type=f32)
                weight = (raised * raised + 1.0).astype(bf16)
                total += jnp.dot(weight, v_v[pl.ds(0, r * rb), lanes], preferred_element_type=f32)
            lown[span, lanes] = total.astype(bf16)

    def across(r):
        return remote(
            lown.at[pl.ds(r * rb, rb)], lx.at[f, pl.ds((r % 2) * rb, rb)], l_send.at[r, 2],
            l_recv.at[f, r % 2], {"feat": partner},
        )

    l_copies = []

    def send_portion(r):
        j, b = r // 2, r % 2
        for k, yy in enumerate((yr, yl)):
            copy = remote(
                lown.at[pl.ds(r * rb, rb)], lx.at[f, pl.ds(b * rb, rb)], l_send.at[r, k], l_recv.at[f, b],
                {"feat": 2 * yy + j},
            )
            copy.start()
            l_copies.append(copy)

        @pl.when(core != j)
        def _():
            across(r).start()

        @pl.when(core == j)
        def _():
            lx[f, pl.ds(b * rb, rb), :] = lown[pl.ds(r * rb, rb), :]

    t_loads[0].wait()
    project(0)
    for copy in k_loads:
        copy.wait()
    t_loads[1].wait()
    project(1)
    own_portion(0)
    add_state(0)
    pl.semaphore_wait(barrier, greetings)
    send_portion(0)
    t_loads[2].wait()
    project(2)
    own_portion(1)
    add_state(1)
    send_portion(1)
    t_loads[3].wait()
    project(3)
    add_state(2)
    add_state(3)

    my_chunk = jnp.clip(z - first_owner, 0, CHUNKS - 1)
    my_rows = pl.ds(pl.multiple_of(my_chunk * CHUNK, CHUNK), CHUNK)

    def to_low(t):
        return remote(st, early.at[jnp.minimum(z, LOW - 1)], p1_send.at[t], e_recv.at[jnp.minimum(z, LOW - 1)], {"seq": t})

    for t in range(LOW, 0, -1):
        @pl.when(z < t)
        def _():
            to_low(t).start()

    def to_owner(k):
        return remote(
            st.at[pl.ds(k * CHUNK, CHUNK)], p1.at[z], p1_send.at[k], p1_recv.at[z], {"seq": first_owner + k}
        )

    def chunks_out():
        for k in range(CHUNKS):
            @pl.when((z != first_owner + k) & (z != n_seq - 1))
            def _():
                to_owner(k).start()

    def gather_low():
        total = jnp.zeros(st.shape, f32)
        for t in range(LOW):
            @pl.when(t < z)
            def _():
                remote(st, early.at[t], p1_send.at[0], e_recv.at[t], {"seq": t}).wait_recv()

            total = total + jnp.where(t < z, early[t].astype(f32), 0.0)
        sx[f] = total.astype(bf16)
        return total

    @pl.when(z > LOW)
    def _():
        chunks_out()

    @pl.when(owns)
    def _():
        p1[z] = st[my_rows, :]

    q_copies = []
    for j in range(2):
        lanes = pl.ds(j * half, half)
        for k, yy in enumerate((yr, yl, yo)):
            q_copies.append(remote(
                qkt.at[pl.ds(0, 2 * DK), lanes], qx.at[f, pl.ds(0, 2 * DK)],
                q_send.at[j * 3 + k], q_recv.at[f], {"feat": 2 * yy + j},
            ))
    q_copies.append(remote(
        qkt.at[pl.ds(0, 2 * DK), pl.ds(pl.multiple_of(other * half, half), half)],
        qx.at[f, pl.ds(0, 2 * DK)], q_send.at[6], q_recv.at[f], {"feat": partner},
    ))
    for copy in q_copies:
        copy.start()
    own_portion(2)
    send_portion(2)
    own_portion(3)
    send_portion(3)
    qx[f, pl.ds(0, 2 * DK), :] = qkt[pl.ds(0, 2 * DK), pl.ds(pl.multiple_of(core * half, half), half)]

    @pl.when(is_last_low)
    def _():
        st[...] = (gather_low() + st[...].astype(f32)).astype(bf16)
        chunks_out()

    for copy in q_loads:
        copy.wait()
    own_w.wait()
    w_copy = remote(wo_v.at[core], wo_v.at[core], w_send, w_recv, {"feat": partner})
    w_copy.start()

    def make_phi(source):
        q = qx[source]
        turned = (
            jnp.dot(e1q_v[...], q, preferred_element_type=f32)
            * jnp.dot(e2q_v[...], q, preferred_element_type=f32)
        )
        for h in range(2):
            phi[source, h] = jnp.transpose(turned[h * FEATS:(h + 1) * FEATS]).astype(bf16)

    make_phi(f)

    def back(c):
        return remote(p2.at[c], sx.at[f, my_rows], p2_send.at[c], p2_recv.at[my_chunk], {"seq": c})

    @pl.when(owns)
    def _():
        total = jnp.zeros((CHUNK, 2 * DV), f32)
        for c in range(first_owner, n_seq):
            @pl.when(z != c - 1)
            def _():
                remote(
                    st.at[pl.ds(0, CHUNK)], p1.at[c - 1], p1_send.at[0], p1_recv.at[c - 1], {"seq": c - 1}
                ).wait_recv()

            total = total + p1[c - 1].astype(f32)
            p2[c] = total.astype(bf16)

            @pl.when(z != c)
            def _():
                back(c).start()

        sx[f, my_rows, :] = p2[z]

    def l_wait(source, b):
        remote(
            lown.at[pl.ds(0, rb)], lx.at[source, pl.ds(b * rb, rb)], l_send.at[0, 0],
            l_recv.at[source, b], {"feat": partner},
        ).wait_recv()

    relays = []

    def relay(b):
        for k, (source, to) in enumerate(((2 * yl, yr), (2 * yr + 1, yl))):
            l_wait(source, b)
            copy = remote(
                lx.at[source, pl.ds(b * rb, rb)], lx.at[source, pl.ds(b * rb, rb)],
                l_relay.at[k, b], l_recv.at[source, b], {"feat": 2 * to + core},
            )
            copy.start()
            relays.append(copy)

    relay(0)

    def phi_of(g, _):
        source = (f + g) % 8
        remote(
            qkt.at[pl.ds(0, 2 * DK), pl.ds(0, half)], qx.at[source, pl.ds(0, 2 * DK)],
            q_send.at[0], q_recv.at[source], {"feat": partner},
        ).wait_recv()
        make_phi(source)
        return 0

    lax.fori_loop(1, 8, phi_of, 0)

    def chunk_in(k, _):
        @pl.when((z != first_owner + k) & (z > LOW))
        def _():
            remote(
                p2.at[0], sx.at[f, pl.ds(pl.multiple_of(k * CHUNK, CHUNK), CHUNK)],
                p2_send.at[0], p2_recv.at[k], {"feat": partner},
            ).wait_recv()
        return 0

    lax.fori_loop(0, CHUNKS, chunk_in, 0)

    @pl.when(z < LOW)
    def _():
        gather_low()

    def s_copy(k, source, target):
        return remote(sx.at[source], sx.at[source], s_send.at[k], s_recv.at[source], {"feat": target})

    def s_wait(source):
        s_copy(0, source, partner).wait_recv()

    near = (2 * yr + core, 2 * yl + core, 2 * yo + core)
    s_copies = [s_copy(k, f, target) for k, target in enumerate((near[2], near[0], near[1], partner))]
    for copy in s_copies:
        copy.start()
    relay(1)
    w_copy.wait_recv()

    def finish(units, first=False):
        for u, (source, b) in enumerate(units):
            span = pl.ds(b * rb, rb)
            for h in range(2):
                lanes = pl.ds(h * DV, DV)
                number = jnp.dot(
                    phi[source, h, span, :], sx[source, :, lanes], preferred_element_type=f32
                ) + lx[source, span, lanes].astype(f32)
                scale = lax.rsqrt(jnp.mean(number * number, axis=-1, keepdims=True) + 4e-6)
                nrm[u, :, lanes] = (number * scale).astype(bf16)
        for b in range(2):
            span = pl.ds(b * rb, rb)
            mine = [(u, source) for u, (source, bb) in enumerate(units) if bb == b]
            for k, which in enumerate((other, core)):
                if mine:
                    term = sum(
                        jnp.dot(
                            nrm[u], wo_v[which, pl.ds(pl.multiple_of(source * 2 * DV, 2 * DV), 2 * DV), :],
                            preferred_element_type=f32,
                        )
                        for u, source in mine
                    )
                    acc[k, span, :] = term if first else acc[k, span, :] + term

    def l_wait_unless_relayed(source, b):
        @pl.when((source != 2 * yl) & (source != 2 * yr + 1))
        def _():
            l_wait(source, b)

    finish([(f, 0), (f, 1)], first=True)
    s_wait(partner)
    for b in range(2):
        l_wait(partner, b)
    finish([(partner, 0), (partner, 1)])
    passed = []

    def s_pass(k):
        s_wait(near[k])
        copy = s_copy(4 + k, near[k], partner)
        copy.start()
        passed.append(copy)

    def sides(sources):
        units = [(source, b) for source in sources for b in range(2)]
        for source, b in units:
            l_wait_unless_relayed(source, b)
        finish(units)

    s_pass(0)
    s_pass(1)
    sides(near[:2])
    s_pass(2)
    beyond = (2 * yr + other, 2 * yl + other, 2 * yo + other)
    s_wait(beyond[0])
    s_wait(beyond[1])
    sides(beyond[:2])
    s_wait(beyond[2])
    out_copies = []
    for b in range(2):
        units = [(near[2], b), (beyond[2], b)]
        for source, _ in units:
            l_wait(source, b)
        finish(units)
        span = pl.ds(b * rb, rb)
        mine = pl.ds(pl.multiple_of(core * half + b * rb, rb), rb)
        outp[span, :] = acc[0, span, :].astype(bf16)
        out_copy = remote(outp.at[span], out.at[mine], o_send.at[b], o_recv.at[b], {"feat": partner})
        out_copy.start()
        out_copies.append(out_copy)
        out[mine, :] = acc[1, span, :].astype(bf16)

    for t in range(LOW, 0, -1):
        @pl.when(z < t)
        def _():
            to_low(t).wait_send()

    for k in range(CHUNKS):
        @pl.when((z >= LOW) & (z != first_owner + k) & (z != n_seq - 1))
        def _():
            to_owner(k).wait_send()

    @pl.when(owns)
    def _():
        for c in range(first_owner, n_seq):
            @pl.when(z != c)
            def _():
                back(c).wait_send()

    for r in range(4):
        @pl.when(core != r // 2)
        def _():
            across(r).wait_send()

    for copy in l_copies + q_copies + [w_copy] + relays + s_copies + passed + out_copies:
        copy.wait_send()
    for b in range(2):
        theirs = pl.ds(pl.multiple_of(other * half + b * rb, rb), rb)
        remote(
            outp.at[pl.ds(b * rb, rb)], out.at[theirs], o_send.at[b], o_recv.at[b], {"feat": partner}
        ).wait_recv()


def local(n_seq, consts, tokens, w_query, w_key, value_weight, w_out):
    rows, deep = tokens.shape
    cols = value_weight.shape[1]
    half = rows // 2
    f32, bf16 = jnp.float32, jnp.bfloat16
    dma = pltpu.SemaphoreType.DMA
    anywhere = pl.BlockSpec(memory_space=pl.ANY)
    vm = pltpu.VMEM
    width = w_query.shape[1]
    return pl.pallas_call(
        functools.partial(kernel, n_seq),
        out_shape=jax.ShapeDtypeStruct((rows, cols), bf16),
        in_specs=[anywhere] * 9,
        out_specs=pl.BlockSpec(memory_space=pltpu.VMEM),
        scratch_shapes=[
            vm((rows, deep), bf16), vm((width, deep), bf16), vm((width, deep), bf16),
            vm((deep, cols), bf16), vm((deep, LANES), bf16), vm((2, 8 * cols, cols), bf16),
            vm((2 * FEATS, LANES), bf16), vm((2 * FEATS, LANES), bf16),
            vm((2 * FEATS, 3 * DK), bf16), vm((2 * FEATS, 3 * DK), bf16),
            vm((rows, LANES), bf16), vm((LANES, rows), bf16), vm((2, LANES, rows), bf16),
            vm((rows, cols), bf16), vm((FEATS, cols), f32), vm((FEATS, cols), bf16),
            vm((n_seq, CHUNK, cols), bf16), vm((n_seq, CHUNK, cols), bf16),
            vm((8, 3 * DK, half), bf16), vm((8, 2, half, FEATS), bf16), vm((8, FEATS, cols), bf16), vm((LOW, FEATS, cols), bf16),
            vm((rows, cols), bf16), vm((8, half, cols), bf16),
            vm((4, half // 2, cols), bf16), vm((2, half, cols), f32), vm((half, cols), bf16),
            dma((12,)), dma((CHUNKS,)), dma((n_seq,)), dma((LOW,)), dma((n_seq,)), dma((CHUNKS,)),
            dma((7,)), dma((8,)), dma, dma,
            dma((4, 3)), dma((2, 2)), dma((8, 2)), dma((7,)), dma((8,)), dma((2,)), dma((2,)),
        ],
        compiler_params=pltpu.CompilerParams(
            collective_id=0, has_side_effects=True, vmem_limit_bytes=56 * 1024 * 1024
        ),
    )(tokens, w_query.T, w_key.T, value_weight, w_out, *consts)


def solution(mesh):
    consts = [
        jnp.asarray(e, jnp.bfloat16)
        for e in (*selectors(2 * DK, ONE, LANES, False), *selectors(0, 2 * DK, 3 * DK, True))
    ]
    placed = (P(("dp", "seq"), None),) + (P(None, "feat"),) * 4

    def run(*args):
        return jax.shard_map(
            functools.partial(local, mesh.shape["seq"], consts),
            mesh=mesh, in_specs=placed, out_specs=P(("dp", "seq"), "feat"), check_vma=False,
        )(*args)

    return run
```

time: 50.5 us -> 44.7 us (0.89)
  the two profiles are of different devices: /device:TPU:1 before, /device:TPU:97 now
where the time goes in v2:
time: 44.7 us; the launch traced here: 44.5 us
  Pallas kernels  42.7 us (96%)
  local copies, waits for them, and re-layouts  1.87 us (4%)
    pallas_call x1, Pallas kernels, local(): pl.pallas_call(functools.partial(kernel, n_seq), out_shape=jax.ShapeDtype...  42.7 us
    unnamed x1, local copies, waits for them, and re-layouts  1.87 us

profile of v2, /device:TPU:97, one launch (start us, length us, event | category | flops | bytes accessed | tf_op | source)
XLA Modules:
  0.0 44.5 jit_solution(18125863854905538539)
XLA Ops:
  0.0 42.7 %shard_map.91 = bf16[1024,256]{1,0:T(8,128)(2,1)} custom-call(bf16[1024,2048]{1,0:T(8,128)(2,1)} %tok.1, bf16[32,2048]{1,0:T(8,128)(2,1)} %bitcast.2, bf16[32,2048]{1,0:T(8,128)(2,1)} %bitcast.3, bf16[2048,256]{1,0:T(8,128)(2,1)} %wv.1, bf16[2048,256]{1,0:T(8,128)(2,1)} %wo.1, bf16[320,128]{1,0:T(8,128)(2,1)} %constant.8.clone.e1k, ...), custom_call_target="tpu_custom_call" | custom-call | tf_op jit(solution)/shard_map/pallas_call | solution.py:486
  42.7 1.9 %copy.11 = bf16[1024,256]{1,0:T(8,128)(2,1)} copy(bf16[1024,256]{1,0:T(8,128)(2,1)} %shard_map.91) | data formatting | bytes 1048576

commit v3 on v2

--- a/solution.py
+++ b/solution.py
@@ -13,9 +13,11 @@
 FEATS = 160
 LANES = 128
 ONE = 64
-CHUNK = 16
+CHUNK = 32
 CHUNKS = FEATS // CHUNK
-LOW = 3
+CHAIN = 8
+HEAD = 3
+FIRST_OWNER = 9
 MESH = pl.DeviceIdType.MESH
 
 
@@ -49,8 +51,8 @@
 def kernel(
     n_seq, tok, wq, wk, wv, wo, e1k, e2k, e1q, e2q, out,
     tok_v, wq_v, wk_v, wv_v, wqk_v, wo_v, e1k_v, e2k_v, e1q_v, e2q_v,
-    qk_v, qkt, kaug, v_v, state, st, p1, p2, qx, phi, sx, early, lown, lx, nrm, acc, outp,
-    load_sem, p1_send, p1_recv, e_recv, p2_send, p2_recv, q_send, q_recv, w_send, w_recv,
+    qk_v, qkt, kaug, v_v, state, st, p1, p2, pair_in, c_in, c_out, qx, phi, sx, lown, lx, nrm, acc, outp,
+    load_sem, ready_sem, p1_send, p1_recv, p2_send, p2_recv, pair_send, pair_recv, c_send, c_recv, e_recv, q_send, q_recv, w_send, w_recv,
     l_send, l_relay, l_recv, s_send, s_recv, o_send, o_recv,
 ):
     f32, bf16 = jnp.float32, jnp.bfloat16
@@ -71,25 +73,35 @@
     barrier = pltpu.get_barrier_semaphore()
     for off in range(1, 8):
         signal(barrier, feat=(f + off) % 8)
-    first_owner = LOW + 1
-    is_low = z <= LOW
-    is_last_low = z == LOW
-    owns = (z >= first_owner) & (z < first_owner + CHUNKS)
-    for t in range(LOW + 1):
-        @pl.when(is_low & (z != t))
+    odd = z % 2 == 1
+    last = CHAIN - 1
+    chained = z < CHAIN
+    owns = (z >= FIRST_OWNER) & (z < FIRST_OWNER + CHUNKS)
+    gives = (z >= HEAD) & (z < n_seq - 1)
+
+    @pl.when(chained & (z >= 1))
+    def _():
+        signal(barrier, seq=z - 1)
+
+    @pl.when(chained & odd & (z >= 3))
+    def _():
+        signal(barrier, seq=z - 2)
+
+    for k in range(CHUNKS):
+        @pl.when((z >= HEAD) & (z != FIRST_OWNER + k))
+        def _():
+            signal(barrier, seq=FIRST_OWNER + k)
+
+    for t in range(CHAIN, n_seq):
+        @pl.when(owns & (z != t) & (not FIRST_OWNER <= t < FIRST_OWNER + CHUNKS))
         def _():
             signal(barrier, seq=t)
 
-    @pl.when(owns)
-    def _():
-        signal(barrier, seq=LOW)
-
-    for t in range(first_owner, n_seq):
-        @pl.when((z > LOW) & (z != t))
-        def _():
-            signal(barrier, seq=t)
-
-    greetings = 7 + jnp.where(is_low, LOW, n_seq - 2 - LOW) + jnp.where(is_last_low, CHUNKS, 0)
+    greetings = 7 + jnp.where(
+        chained,
+        (z < last).astype(jnp.int32) + (odd & (z < last - 1)).astype(jnp.int32),
+        jnp.where(owns, n_seq - HEAD - 1, CHUNKS),
+    )
 
     def load(src, dst, k):
         return pltpu.make_async_copy(src, dst, load_sem.at[k])
@@ -197,51 +209,53 @@
     own_portion(0)
     add_state(0)
     pl.semaphore_wait(barrier, greetings)
+    for t in range(HEAD, CHAIN):
+        @pl.when(owns)
+        def _():
+            signal(ready_sem, seq=t)
+
     send_portion(0)
     t_loads[2].wait()
     project(2)
-    own_portion(1)
     add_state(1)
-    send_portion(1)
     t_loads[3].wait()
     project(3)
+
+    def q_copy(n, j, source, target):
+        return remote(
+            qkt.at[pl.ds(0, 2 * DK), pl.ds(pl.multiple_of(j * half, half), half)], qx.at[source, pl.ds(0, 2 * DK)],
+            q_send.at[n], q_recv.at[source], {"feat": target},
+        )
+
+    q_copies = [q_copy(2 * j + k, j, f, 2 * yy + j) for j in range(2) for k, yy in enumerate((yr, yl))]
+    q_copies.append(q_copy(4, other, f, partner))
+    for copy in q_copies:
+        copy.start()
     add_state(2)
     add_state(3)
 
-    my_chunk = jnp.clip(z - first_owner, 0, CHUNKS - 1)
+    my_chunk = jnp.clip(z - FIRST_OWNER, 0, CHUNKS - 1)
     my_rows = pl.ds(pl.multiple_of(my_chunk * CHUNK, CHUNK), CHUNK)
 
-    def to_low(t):
-        return remote(st, early.at[jnp.minimum(z, LOW - 1)], p1_send.at[t], e_recv.at[jnp.minimum(z, LOW - 1)], {"seq": t})
-
-    for t in range(LOW, 0, -1):
-        @pl.when(z < t)
-        def _():
-            to_low(t).start()
+    def pair_copy():
+        return remote(st, pair_in, pair_send, pair_recv, {"seq": z + 1})
+
+    @pl.when(chained & jnp.logical_not(odd))
+    def _():
+        pair_copy().start()
 
     def to_owner(k):
         return remote(
-            st.at[pl.ds(k * CHUNK, CHUNK)], p1.at[z], p1_send.at[k], p1_recv.at[z], {"seq": first_owner + k}
+            st.at[pl.ds(k * CHUNK, CHUNK)], p1.at[z], p1_send.at[k], p1_recv.at[z], {"seq": FIRST_OWNER + k}
         )
 
     def chunks_out():
         for k in range(CHUNKS):
-            @pl.when((z != first_owner + k) & (z != n_seq - 1))
+            @pl.when(z != FIRST_OWNER + k)
             def _():
                 to_owner(k).start()
 
-    def gather_low():
-        total = jnp.zeros(st.shape, f32)
-        for t in range(LOW):
-            @pl.when(t < z)
-            def _():
-                remote(st, early.at[t], p1_send.at[0], e_recv.at[t], {"seq": t}).wait_recv()
-
-            total = total + jnp.where(t < z, early[t].astype(f32), 0.0)
-        sx[f] = total.astype(bf16)
-        return total
-
-    @pl.when(z > LOW)
+    @pl.when(gives & jnp.logical_not(chained))
     def _():
         chunks_out()
 
@@ -249,30 +263,13 @@
     def _():
         p1[z] = st[my_rows, :]
 
-    q_copies = []
-    for j in range(2):
-        lanes = pl.ds(j * half, half)
-        for k, yy in enumerate((yr, yl, yo)):
-            q_copies.append(remote(
-                qkt.at[pl.ds(0, 2 * DK), lanes], qx.at[f, pl.ds(0, 2 * DK)],
-                q_send.at[j * 3 + k], q_recv.at[f], {"feat": 2 * yy + j},
-            ))
-    q_copies.append(remote(
-        qkt.at[pl.ds(0, 2 * DK), pl.ds(pl.multiple_of(other * half, half), half)],
-        qx.at[f, pl.ds(0, 2 * DK)], q_send.at[6], q_recv.at[f], {"feat": partner},
-    ))
-    for copy in q_copies:
-        copy.start()
+    own_portion(1)
+    send_portion(1)
     own_portion(2)
     send_portion(2)
     own_portion(3)
     send_portion(3)
     qx[f, pl.ds(0, 2 * DK), :] = qkt[pl.ds(0, 2 * DK), pl.ds(pl.multiple_of(core * half, half), half)]
-
-    @pl.when(is_last_low)
-    def _():
-        st[...] = (gather_low() + st[...].astype(f32)).astype(bf16)
-        chunks_out()
 
     for copy in q_loads:
         copy.wait()
@@ -291,13 +288,83 @@
 
     make_phi(f)
 
+    near = (2 * yr + core, 2 * yl + core, 2 * yo + core)
+    beyond = (2 * yr + other, 2 * yl + other, 2 * yo + other)
+
+    def piece(k):
+        return pl.ds(pl.multiple_of(k * CHUNK, CHUNK), CHUNK)
+
+    def s_piece(n, k, source, target):
+        return remote(
+            sx.at[source, piece(k)], sx.at[source, piece(k)], s_send.at[n, k], s_recv.at[source, k],
+            {"feat": target},
+        )
+
+    def to_odd(k):
+        return remote(c_out.at[piece(k)], c_in.at[piece(k)], c_send.at[0, k], c_recv.at[k], {"seq": z + 2})
+
+    def to_even(k):
+        return remote(c_out.at[piece(k)], sx.at[f, piece(k)], c_send.at[1, k], e_recv.at[k], {"seq": z + 1})
+
+    def chain():
+        @pl.when(z == 0)
+        def _():
+            sx[f] = jnp.zeros(sx.shape[1:], bf16)
+
+        @pl.when(odd)
+        def _():
+            pair_copy().wait_recv()
+
+        def step(k, _):
+            @pl.when(odd)
+            def _():
+                @pl.when(z >= 3)
+                def _():
+                    to_odd(k).wait_recv()
+
+                before = jnp.where(z >= 3, c_in[piece(k), :].astype(f32), 0.0) + pair_in[piece(k), :].astype(f32)
+                c_out[piece(k), :] = (before + st[piece(k), :].astype(f32)).astype(bf16)
+                sx[f, piece(k), :] = before.astype(bf16)
+
+                @pl.when(z < last - 1)
+                def _():
+                    to_odd(k).start()
+
+                @pl.when(z < last)
+                def _():
+                    to_even(k).start()
+
+            @pl.when(jnp.logical_not(odd) & (z >= 2))
+            def _():
+                to_even(k).wait_recv()
+
+            for n, target in enumerate((near[0], near[1], partner)):
+                s_piece(n, k, f, target).start()
+            return 0
+
+        lax.fori_loop(0, CHUNKS, step, 0)
+
+    @pl.when(chained)
+    def _():
+        @pl.when(z > HEAD)
+        def _():
+            pl.semaphore_wait(ready_sem, CHUNKS)
+            chunks_out()
+
+        chain()
+
+        @pl.when(z == HEAD)
+        def _():
+            pl.semaphore_wait(ready_sem, CHUNKS)
+            st[...] = c_out[...]
+            chunks_out()
+
     def back(c):
         return remote(p2.at[c], sx.at[f, my_rows], p2_send.at[c], p2_recv.at[my_chunk], {"seq": c})
 
-    @pl.when(owns)
-    def _():
+    def own_chunk():
         total = jnp.zeros((CHUNK, 2 * DV), f32)
-        for c in range(first_owner, n_seq):
+        for c in range(HEAD + 1, n_seq):
             @pl.when(z != c - 1)
             def _():
                 remote(
@@ -305,13 +372,28 @@
                 ).wait_recv()
 
             total = total + p1[c - 1].astype(f32)
-            p2[c] = total.astype(bf16)
-
-            @pl.when(z != c)
-            def _():
-                back(c).start()
+            if c >= CHAIN:
+                p2[c] = total.astype(bf16)
+
+                @pl.when(z != c)
+                def _():
+                    back(c).start()
 
         sx[f, my_rows, :] = p2[z]
+
+    def from_owners():
+        def step(k, _):
+            @pl.when(z != FIRST_OWNER + k)
+            def _():
+                remote(
+                    p2.at[0], sx.at[f, piece(k)], p2_send.at[0], p2_recv.at[k], {"feat": partner}
+                ).wait_recv()
+
+            for n, target in enumerate((near[0], near[1], partner)):
+                s_piece(n, k, f, target).start()
+            return 0
+
+        lax.fori_loop(0, CHUNKS, step, 0)
 
     def l_wait(source, b):
         remote(
@@ -320,56 +402,71 @@
         ).wait_recv()
 
     relays = []
+    onward = ((2 * yl, yr), (2 * yr + 1, yl))
+    for k, (source, to) in enumerate(onward):
+        q_copy(0, 0, source, partner).wait_recv()
+        copy = remote(
+            qx.at[source, pl.ds(0, 2 * DK)], qx.at[source, pl.ds(0, 2 * DK)],
+            q_send.at[5 + k], q_recv.at[source], {"feat": 2 * to + core},
+        )
+        copy.start()
+        relays.append(copy)
+
+    def l_onward(k, b):
+        source, to = onward[k]
+        span = pl.ds(b * rb, rb)
+        return remote(
+            lx.at[source, span], lx.at[source, span], l_relay.at[k, b], l_recv.at[source, b],
+            {"feat": 2 * to + core},
+        )
 
     def relay(b):
-        for k, (source, to) in enumerate(((2 * yl, yr), (2 * yr + 1, yl))):
+        for k, (source, to) in enumerate(onward):
             l_wait(source, b)
-            copy = remote(
-                lx.at[source, pl.ds(b * rb, rb)], lx.at[source, pl.ds(b * rb, rb)],
-                l_relay.at[k, b], l_recv.at[source, b], {"feat": 2 * to + core},
-            )
-            copy.start()
-            relays.append(copy)
+            l_onward(k, b).start()
+
+    def phi_of(source):
+        @pl.when((source != 2 * yl) & (source != 2 * yr + 1))
+        def _():
+            q_copy(0, 0, source, partner).wait_recv()
+
+        make_phi(source)
+
+    def phi_near(g, _):
+        phi_of(jnp.where(g < 4, 2 * jnp.where(g < 2, yr, yl) + g % 2, partner))
+        return 0
+
+    def phi_far(g, _):
+        phi_of(2 * yo + g)
+        return 0
+
+    lax.fori_loop(0, 5, phi_near, 0)
+
+    @pl.when(owns)
+    def _():
+        own_chunk()
 
     relay(0)
-
-    def phi_of(g, _):
-        source = (f + g) % 8
-        remote(
-            qkt.at[pl.ds(0, 2 * DK), pl.ds(0, half)], qx.at[source, pl.ds(0, 2 * DK)],
-            q_send.at[0], q_recv.at[source], {"feat": partner},
-        ).wait_recv()
-        make_phi(source)
-        return 0
-
-    lax.fori_loop(1, 8, phi_of, 0)
-
-    def chunk_in(k, _):
-        @pl.when((z != first_owner + k) & (z > LOW))
-        def _():
-            remote(
-                p2.at[0], sx.at[f, pl.ds(pl.multiple_of(k * CHUNK, CHUNK), CHUNK)],
-                p2_send.at[0], p2_recv.at[k], {"feat": partner},
-            ).wait_recv()
-        return 0
-
-    lax.fori_loop(0, CHUNKS, chunk_in, 0)
-
-    @pl.when(z < LOW)
-    def _():
-        gather_low()
-
-    def s_copy(k, source, target):
-        return remote(sx.at[source], sx.at[source], s_send.at[k], s_recv.at[source], {"feat": target})
+    @pl.when(jnp.logical_not(chained))
+    def _():
+        from_owners()
+
+    relay(1)
 
     def s_wait(source):
-        s_copy(0, source, partner).wait_recv()
-
-    near = (2 * yr + core, 2 * yl + core, 2 * yo + core)
-    s_copies = [s_copy(k, f, target) for k, target in enumerate((near[2], near[0], near[1], partner))]
-    for copy in s_copies:
-        copy.start()
-    relay(1)
+        for k in range(CHUNKS):
+            s_piece(0, k, source, partner).wait_recv()
+
+    def s_pass(n):
+        for k in range(CHUNKS):
+            s_piece(0, k, near[n], partner).wait_recv()
+            if n < 2:
+                @pl.when(core == 1 - n)
+                def _():
+                    s_piece(6, k, near[n], near[1 - n]).start()
+            s_piece(3 + n, k, near[n], partner).start()
+
+    lax.fori_loop(0, 2, phi_far, 0)
     w_copy.wait_recv()
 
     def finish(units, first=False):
@@ -406,14 +503,6 @@
     for b in range(2):
         l_wait(partner, b)
     finish([(partner, 0), (partner, 1)])
-    passed = []
-
-    def s_pass(k):
-        s_wait(near[k])
-        copy = s_copy(4 + k, near[k], partner)
-        copy.start()
-        passed.append(copy)
-
     def sides(sources):
         units = [(source, b) for source in sources for b in range(2)]
         for source, b in units:
@@ -424,7 +513,6 @@
     s_pass(1)
     sides(near[:2])
     s_pass(2)
-    beyond = (2 * yr + other, 2 * yl + other, 2 * yo + other)
     s_wait(beyond[0])
     s_wait(beyond[1])
     sides(beyond[:2])
@@ -443,35 +531,50 @@
         out_copies.append(out_copy)
         out[mine, :] = acc[1, span, :].astype(bf16)
 
-    for t in range(LOW, 0, -1):
-        @pl.when(z < t)
-        def _():
-            to_low(t).wait_send()
-
-    for k in range(CHUNKS):
-        @pl.when((z >= LOW) & (z != first_owner + k) & (z != n_seq - 1))
-        def _():
-            to_owner(k).wait_send()
-
-    @pl.when(owns)
-    def _():
-        for c in range(first_owner, n_seq):
-            @pl.when(z != c)
-            def _():
-                back(c).wait_send()
-
-    for r in range(4):
-        @pl.when(core != r // 2)
-        def _():
-            across(r).wait_send()
-
-    for copy in l_copies + q_copies + [w_copy] + relays + s_copies + passed + out_copies:
-        copy.wait_send()
-    for b in range(2):
-        theirs = pl.ds(pl.multiple_of(other * half + b * rb, rb), rb)
-        remote(
-            outp.at[pl.ds(b * rb, rb)], out.at[theirs], o_send.at[b], o_recv.at[b], {"feat": partner}
-        ).wait_recv()
+    with jax.named_scope('tail_sends'):
+        @pl.when(chained & jnp.logical_not(odd))
+        def _():
+            pair_copy().wait_send()
+
+        for k in range(CHUNKS):
+            @pl.when(chained & odd & (z < last - 1))
+            def _():
+                to_odd(k).wait_send()
+
+            @pl.when(chained & odd & (z < last))
+            def _():
+                to_even(k).wait_send()
+
+            @pl.when(gives & (z != FIRST_OWNER + k))
+            def _():
+                to_owner(k).wait_send()
+
+        @pl.when(owns)
+        def _():
+            for c in range(CHAIN, n_seq):
+                @pl.when(z != c)
+                def _():
+                    back(c).wait_send()
+
+        for r in range(4):
+            @pl.when(core != r // 2)
+            def _():
+                across(r).wait_send()
+
+        for copy in l_copies + q_copies + [w_copy] + relays + out_copies:
+            copy.wait_send()
+        for k in range(2):
+            for b in range(2):
+                l_onward(k, b).wait_send()
+        for n, source in enumerate((f, f, f, near[0], near[1], near[2], f)):
+            for k in range(CHUNKS):
+                s_piece(n, k, source, partner).wait_send()
+    with jax.named_scope('tail_recv'):
+        for b in range(2):
+            theirs = pl.ds(pl.multiple_of(other * half + b * rb, rb), rb)
+            remote(
+                outp.at[pl.ds(b * rb, rb)], out.at[theirs], o_send.at[b], o_recv.at[b], {"feat": partner}
+            ).wait_recv()
 
 
 def local(n_seq, consts, tokens, w_query, w_key, value_weight, w_out):
@@ -483,9 +586,9 @@
     anywhere = pl.BlockSpec(memory_space=pl.ANY)
     vm = pltpu.VMEM
     width = w_query.shape[1]
-    return pl.pallas_call(
+    mixed = pl.pallas_call(
         functools.partial(kernel, n_seq),
-        out_shape=jax.ShapeDtypeStruct((rows, cols), bf16),
+        out_shape=pltpu.VMEM((rows, cols), bf16),
         in_specs=[anywhere] * 9,
         out_specs=pl.BlockSpec(memory_space=pltpu.VMEM),
         scratch_shapes=[
@@ -496,17 +599,20 @@
             vm((rows, LANES), bf16), vm((LANES, rows), bf16), vm((2, LANES, rows), bf16),
             vm((rows, cols), bf16), vm((FEATS, cols), f32), vm((FEATS, cols), bf16),
             vm((n_seq, CHUNK, cols), bf16), vm((n_seq, CHUNK, cols), bf16),
-            vm((8, 3 * DK, half), bf16), vm((8, 2, half, FEATS), bf16), vm((8, FEATS, cols), bf16), vm((LOW, FEATS, cols), bf16),
+            vm((FEATS, cols), bf16), vm((FEATS, cols), bf16), vm((FEATS, cols), bf16),
+            vm((8, 3 * DK, half), bf16), vm((8, 2, half, FEATS), bf16), vm((8, FEATS, cols), bf16),
             vm((rows, cols), bf16), vm((8, half, cols), bf16),
             vm((4, half // 2, cols), bf16), vm((2, half, cols), f32), vm((half, cols), bf16),
-            dma((12,)), dma((CHUNKS,)), dma((n_seq,)), dma((LOW,)), dma((n_seq,)), dma((CHUNKS,)),
+            dma((12,)), pltpu.SemaphoreType.REGULAR,
+            dma((CHUNKS,)), dma((n_seq,)), dma((n_seq,)), dma((CHUNKS,)), dma, dma, dma((2, CHUNKS)), dma((CHUNKS,)), dma((CHUNKS,)),
             dma((7,)), dma((8,)), dma, dma,
-            dma((4, 3)), dma((2, 2)), dma((8, 2)), dma((7,)), dma((8,)), dma((2,)), dma((2,)),
+            dma((4, 3)), dma((2, 2)), dma((8, 2)), dma((7, CHUNKS)), dma((8, CHUNKS)), dma((2,)), dma((2,)),
         ],
         compiler_params=pltpu.CompilerParams(
             collective_id=0, has_side_effects=True, vmem_limit_bytes=56 * 1024 * 1024
         ),
     )(tokens, w_query.T, w_key.T, value_weight, w_out, *consts)
+    return mixed
 
 
 def solution(mesh):

time: 44.7 us -> 41.4 us (0.926)
  the two profiles are of different devices: /device:TPU:97 before, /device:TPU:481 now
where the time goes in v3:
time: 41.4 us; the launch traced here: 41.3 us
  Pallas kernels  40.5 us (98%)
  local copies, waits for them, and re-layouts  0.8 us (2%)
    pallas_call x1, Pallas kernels, local(): pl.pallas_call(functools.partial(kernel, n_seq), out_shape=pltpu.VMEM((ro...  40.5 us

profile of v3, /device:TPU:481, one launch (start us, length us, event | category | flops | bytes accessed | tf_op | source)
XLA Modules:
  0.0 41.3 jit_solution(11045541006149855023)
XLA Ops:
  0.0 40.5 %shard_map.91 = bf16[1024,256]{1,0:T(8,128)(2,1)S(1)} custom-call(bf16[1024,2048]{1,0:T(8,128)(2,1)} %tok.1, bf16[32,2048]{1,0:T(8,128)(2,1)} %bitcast.2, bf16[32,2048]{1,0:T(8,128)(2,1)} %bitcast.3, bf16[2048,256]{1,0:T(8,128)(2,1)} %wv.1, bf16[2048,256]{1,0:T(8,128)(2,1)} %wo.1, bf16[320,128]{1,0:T(8,128)(2,1)} %constant.8.clone.e1k, ...), custom_call_target="tpu_custom_call" | custom-call | tf_op jit(solution)/shard_map/pallas_call | solution.py:589
  40.5 0.8 %copy.11 = bf16[1024,256]{1,0:T(8,128)(2,1)} copy(bf16[1024,256]{1,0:T(8,128)(2,1)S(1)} %shard_map.91) | data formatting | bytes 1048576

commit v4 on v3

--- a/solution.py
+++ b/solution.py
@@ -17,7 +17,7 @@
 CHUNKS = FEATS // CHUNK
 CHAIN = 8
 HEAD = 3
-FIRST_OWNER = 9
+FIRST_OWNER = 10
 MESH = pl.DeviceIdType.MESH
 
 
@@ -440,18 +440,26 @@
         phi_of(2 * yo + g)
         return 0
 
-    lax.fori_loop(0, 5, phi_near, 0)
+    @pl.when(jnp.logical_not(chained))
+    def _():
+        lax.fori_loop(0, 5, phi_near, 0)
+
+    relay(0)
 
     @pl.when(owns)
     def _():
         own_chunk()
 
-    relay(0)
+    relay(1)
+
+    @pl.when(chained)
+    def _():
+        lax.fori_loop(0, 5, phi_near, 0)
+
     @pl.when(jnp.logical_not(chained))
     def _():
         from_owners()
 
-    relay(1)
 
     def s_wait(source):
         for k in range(CHUNKS):

time: 41.4 us -> 40.9 us (0.988)
  the two profiles are of different devices: /device:TPU:481 before, /device:TPU:1 now
where the time goes in v4:
time: 40.9 us; the launch traced here: 40.4 us
  Pallas kernels  39.6 us (97%)
  local copies, waits for them, and re-layouts  0.8 us (2%)
    pallas_call x1, Pallas kernels, local(): pl.pallas_call(functools.partial(kernel, n_seq), out_shape=pltpu.VMEM((ro...  39.6 us

profile of v4, /device:TPU:1, one launch (start us, length us, event | category | flops | bytes accessed | tf_op | source)
XLA Modules:
  0.0 40.4 jit_solution(14932711858906656160)
XLA Ops:
  0.0 39.6 %shard_map.91 = bf16[1024,256]{1,0:T(8,128)(2,1)S(1)} custom-call(bf16[1024,2048]{1,0:T(8,128)(2,1)} %tok.1, bf16[32,2048]{1,0:T(8,128)(2,1)} %bitcast.2, bf16[32,2048]{1,0:T(8,128)(2,1)} %bitcast.3, bf16[2048,256]{1,0:T(8,128)(2,1)} %wv.1, bf16[2048,256]{1,0:T(8,128)(2,1)} %wo.1, bf16[320,128]{1,0:T(8,128)(2,1)} %constant.8.clone.e1k, ...), custom_call_target="tpu_custom_call" | custom-call | tf_op jit(solution)/shard_map/pallas_call | solution.py:597
  39.6 0.8 %copy.11 = bf16[1024,256]{1,0:T(8,128)(2,1)} copy(bf16[1024,256]{1,0:T(8,128)(2,1)S(1)} %shard_map.91) | data formatting | bytes 1048576
